TPU v7x, 32 devices: a whole 2x2x4 slice. The times are simulated.
32 devices in a mesh: ctx: 2 (over y), dp: 16 (over z, x, core).
Axes of the slice: x: 2, y: 2, z: 4, core: 2. Of those that a mesh axis runs over, the one named last changes fastest.
Arguments:
- queries: bfloat16 [16, 256, 1024], P('dp', 'ctx'), may hold values from -20 to 20
- keys: bfloat16 [16, 256, 1024], P('dp', 'ctx'), may hold values from -4 to 4
- values: bfloat16 [16, 256, 1024], P('dp', 'ctx'), may hold values from -6 to 6
- d_mixed: bfloat16 [16, 256, 1024], P('dp', 'ctx'), may hold values from -6 to 6
- series_ids: int32 [16, 256], P('dp', 'ctx'), may hold values from 0 to 3, never falling along the last dimension, each value on 1 to 192 neighbouring positions
- variate_ids: int32 [16, 256], P('dp', 'ctx'), may hold values from 0 to 3
- variate_bias: float32 [2, 16], replicated, may hold values from -4 to 4
- w_out: bfloat16 [1024, 1024], P('dp'), may hold values from -0.1875 to 0.1875
Outputs:
- mixed: bfloat16 [16, 256, 1024], P('dp', 'ctx')
- q_grad: bfloat16 [16, 256, 1024], P('dp', 'ctx')
- k_grad: bfloat16 [16, 256, 1024], P('dp', 'ctx')
- v_grad: bfloat16 [16, 256, 1024], P('dp', 'ctx')
- w_grad: float32 [1024, 1024], P('dp')
- bias_grad: float32 [2, 16], replicated
Inputs may be any that keep to these rules, and one draw needn't show every extreme that they name: `series_ids`: within a packed row series numbers never fall; each series spans 1 to 192 consecutive tokens and some series spans exactly 192.
All inputs are finite; a program needn't handle non-finite values.
Results may differ from a plain program's by a relative error of at most 0.015.
Values may be sent and summed in bfloat16 or wider, within the bound.
No kernel may reach another device: no remote copies, remote signals or barrier semaphores. Data moves between devices by JAX's collectives and lax.ppermute only.
A program may use at most 128 MiB of HBM per device.

v0:
```python
import jax
import jax.numpy as jnp
from jax import lax
from jax.sharding import PartitionSpec as P

HEADS = 16
HEAD_DIM = 64
NEG = -1e30
group_width = 4


def shifted_2(shard, axis, by):
    count = lax.axis_size(axis)
    pairs = [(i, i + by) for i in range(count) if 0 <= i + by < count]
    return lax.ppermute(shard, axis, pairs)


def split_heads(block):
    rows = block.shape[0]
    return block.reshape(rows, HEADS // group_width, group_width, HEAD_DIM).transpose(1, 0, 2, 3)


def merge_heads(block):
    rows = block.shape[1]
    return block.transpose(1, 0, 2, 3).reshape(rows, HEADS * HEAD_DIM)


def stats_groups(rows_heads):
    count = rows_heads.shape[0]
    return rows_heads.reshape(count, HEADS // group_width, group_width).transpose(1, 2, 0)


def scored(q_group, k_group, bias_group, q_tag, k_tag, q_var, k_var):
    raw = jnp.einsum(
        "qhd,khd->hqk", q_group, k_group, preferred_element_type=jnp.float32
    ) * HEAD_DIM ** (-0.5)
    same = (q_var[:, None] == k_var[None, :])[None]
    allowed = (q_tag[:, None] == k_tag[None, :])[None]
    shifted = raw + jnp.where(same, bias_group[0][:, None, None], bias_group[1][:, None, None])
    return (jnp.where(allowed, shifted, NEG), allowed, same)


def joined(pieces):
    return [jnp.concatenate(items, axis=0) for items in zip(*pieces)]


def on_device(queries, keys, values, d_mixed, series_ids, variate_ids, variate_bias, w_out):
    query = queries[0]
    key_rows = keys[0]
    value_rows = values[0]
    upstream = d_mixed[0]
    tags = series_ids[0] + 1
    variety = variate_ids[0]
    tok = query.shape[0]
    n_ctx = lax.axis_size("ctx")
    most = tok * n_ctx // 2 + tok // 2
    reach = min((most - 2) // tok + 1, n_ctx - 1)
    scale = HEAD_DIM ** (-0.5)
    w_full = lax.all_gather(w_out, "dp", axis=0, tiled=True)
    d_context = lax.dot_general(
        upstream, w_full, (((1,), (1,)), ((), ())), preferred_element_type=jnp.float32
    ).astype(jnp.bfloat16)
    bias_groups = variate_bias.reshape(2, HEADS // group_width, group_width).transpose(1, 0, 2)
    pieces = [(key_rows, value_rows, tags, variety)]
    for dist in range(1, reach + 1):
        pieces.append(shifted_2((key_rows, value_rows, tags, variety), "ctx", dist))
        pieces.append(shifted_2((key_rows, value_rows, tags, variety), "ctx", -dist))
    key_set, value_set, key_tags, key_vars = joined(pieces)
    q_groups = split_heads(query)
    k_groups = split_heads(key_set)
    v_groups = split_heads(value_set)

    def forward_group(items):
        q_group, k_group, v_group, bias_group = items
        scores, allowed, same = scored(
            q_group, k_group, bias_group, tags, key_tags, variety, key_vars
        )
        top = jnp.max(scores, axis=2, keepdims=True)
        total = jnp.sum(jnp.where(allowed, jnp.exp(scores - top), 0.0), axis=2, keepdims=True)
        lse = top + jnp.log(total)
        probs = jnp.where(allowed, jnp.exp(scores - lse), 0.0)
        context = jnp.einsum(
            "hqk,khd->qhd", probs.astype(jnp.bfloat16), v_group, preferred_element_type=jnp.float32
        )
        return (context, lse[:, :, 0], probs)

    context_groups, lse_groups, prob_groups = lax.map(
        forward_group, (q_groups, k_groups, v_groups, bias_groups)
    )
    context = merge_heads(context_groups)
    context_bf = context.astype(jnp.bfloat16)
    delta_rows = jnp.sum(
        (d_context.astype(jnp.float32) * context).reshape(tok, HEADS, HEAD_DIM), axis=2
    )
    lse_rows = lse_groups.transpose(2, 0, 1).reshape(tok, HEADS)
    d_groups = split_heads(d_context)
    delta_groups = stats_groups(delta_rows)

    def query_group(items):
        k_group, v_group, d_group, probs, delta_group, bias_group = items
        same = (variety[:, None] == key_vars[None, :])[None]
        dprob = jnp.einsum("qhd,khd->hqk", d_group, v_group, preferred_element_type=jnp.float32)
        dscore = probs * (dprob - delta_group[:, :, None])
        grads = (
            jnp.einsum(
                "hqk,khd->qhd",
                dscore.astype(jnp.bfloat16),
                k_group,
                preferred_element_type=jnp.float32,
            )
            * scale
        )
        sums = jnp.stack(
            [
                jnp.sum(jnp.where(same, dscore, 0.0), axis=(1, 2)),
                jnp.sum(jnp.where(same, 0.0, dscore), axis=(1, 2)),
            ]
        )
        return (grads, sums)

    q_grads, sum_groups = lax.map(
        query_group, (k_groups, v_groups, d_groups, prob_groups, delta_groups, bias_groups)
    )
    bias_terms = sum_groups.transpose(1, 0, 2).reshape(2, HEADS)
    front = [(query, d_context, tags, variety)]
    numbers = [(lse_rows, delta_rows)]
    for dist in range(1, reach + 1):
        front.append(shifted_2((query, d_context, tags, variety), "ctx", dist))
        numbers.append(shifted_2((lse_rows, delta_rows), "ctx", dist))
        front.append(shifted_2((query, d_context, tags, variety), "ctx", -dist))
        numbers.append(shifted_2((lse_rows, delta_rows), "ctx", -dist))
    remote_q, remote_d, remote_tags, remote_vars = joined(front)
    remote_lse, remote_delta = joined(numbers)

    def key_group(items):
        q_group, d_group, lse_group, delta_group, k_group, v_group, bias_group = items
        scores, allowed, same = scored(
            q_group, k_group, bias_group, remote_tags, tags, remote_vars, variety
        )
        probs = jnp.where(allowed, jnp.exp(scores - lse_group[:, :, None]), 0.0)
        dprob = jnp.einsum("qhd,khd->hqk", d_group, v_group, preferred_element_type=jnp.float32)
        dscore = probs * (dprob - delta_group[:, :, None])
        k_grad = (
            jnp.einsum(
                "hqk,qhd->khd",
                dscore.astype(jnp.bfloat16),
                q_group,
                preferred_element_type=jnp.float32,
            )
            * scale
        )
        v_grad = jnp.einsum(
            "hqk,qhd->khd", probs.astype(jnp.bfloat16), d_group, preferred_element_type=jnp.float32
        )
        return (k_grad, v_grad)

    k_grads, v_grads = lax.map(
        key_group,
        (
            split_heads(remote_q),
            split_heads(remote_d),
            stats_groups(remote_lse),
            stats_groups(remote_delta),
            split_heads(key_rows),
            split_heads(value_rows),
            bias_groups,
        ),
    )
    q_out = merge_heads(q_grads).astype(jnp.bfloat16)
    k_out = merge_heads(k_grads).astype(jnp.bfloat16)
    v_out = merge_heads(v_grads).astype(jnp.bfloat16)
    mixed = jnp.dot(context_bf, w_full, preferred_element_type=jnp.float32).astype(jnp.bfloat16)
    partial_rows = lax.psum_scatter(
        lax.dot_general(
            context_bf, upstream, (((0,), (0,)), ((), ())), preferred_element_type=jnp.float32
        ),
        "dp",
        scatter_dimension=0,
        tiled=True,
    )
    w_grad = lax.psum(partial_rows, "ctx")
    bias_grad = lax.psum(bias_terms, ("ctx", "dp"))
    return (mixed[None], q_out[None], k_out[None], v_out[None], w_grad, bias_grad)


def solution(mesh):
    return jax.shard_map(
        on_device,
        mesh=mesh,
        in_specs=(
            P("dp", "ctx", None),
            P("dp", "ctx", None),
            P("dp", "ctx", None),
            P("dp", "ctx", None),
            P("dp", "ctx"),
            P("dp", "ctx"),
            P(),
            P("dp", None),
        ),
        out_specs=(
            P("dp", "ctx", None),
            P("dp", "ctx", None),
            P("dp", "ctx", None),
            P("dp", "ctx", None),
            P("dp", None),
            P(),
        ),
        check_vma=False,
    )
```

profile of v0, /device:TPU:0, one launch (start us, length us, event | category | flops | bytes accessed | tf_op | source)
XLA Modules:
  0.0 179.6 jit_solution(639569366921417282)
XLA Ops:
  8.4 4.9 %collective-permute-start = (bf16[128,1024]{0,1:T(8,128)(2,1)S(1)}, bf16[128,1024]{0,1:T(8,128)(2,1)S(1)}, u32[]{:S(2)}, u32[]{:S(2)}) collective-permute-start(bf16[128,1024]{0,1:T(8,128)(2,1)S(1)} %bitcast.263), channel_id=1, source_target_pairs={{0,16},{1,17},{2,18},{3,19},{4,20},{5,21},{6,22},{7,23},{8,24},{9,... | collective-permute-start | bytes 786440 | tf_op jit(solution)/shard_map/ppermute | solution.py:15
  14.7 4.6 %collective-permute-start.4 = (bf16[128,1024]{1,0:T(8,128)(2,1)}, bf16[128,1024]{1,0:T(8,128)(2,1)S(1)}, u32[]{:S(2)}, u32[]{:S(2)}) collective-permute-start(bf16[128,1024]{1,0:T(8,128)(2,1)} %bitcast.278), channel_id=1, source_target_pairs={{0,16},{1,17},{2,18},{3,19},{4,20},{5,21},{6,22},{7,23},{8,24},{9,... | collective-permute-start | bytes 786440 | tf_op jit(solution)/shard_map/ppermute | solution.py:15
  24.6 4.4 %collective-permute-start.6 = (s32[128]{0:T(128)}, s32[128]{0:T(128)S(1)}, u32[]{:S(2)}, u32[]{:S(2)}) collective-permute-start(s32[128]{0:T(128)} %bitcast.285), channel_id=1, source_target_pairs={{0,16},{1,17},{2,18},{3,19},{4,20},{5,21},{6,22},{7,23},{8,24},{9,... | collective-permute-start | bytes 1544 | tf_op jit(solution)/shard_map/ppermute | solution.py:15
  32.8 2.8 %collective-permute-done.7 = s32[128]{0:T(128)S(1)} collective-permute-done((s32[128]{0:T(128)S(1)}, s32[128]{0:T(128)S(1)}, u32[]{:S(2)}, u32[]{:S(2)}) %collective-permute-start.7) | collective-permute-done | bytes 544 | tf_op jit(solution)/shard_map/ppermute | solution.py:15
  37.8 2.0 %collective-permute-done.5 = bf16[128,1024]{1,0:T(8,128)(2,1)S(1)} collective-permute-done((bf16[128,1024]{1,0:T(8,128)(2,1)S(1)}, bf16[128,1024]{1,0:T(8,128)(2,1)S(1)}, u32[]{:S(2)}, u32[]{:S(2)}) %collective-permute-start.5) | collective-permute-done | bytes 262176 | tf_op jit(solution)/shard_map/ppermute | solution.py:15
  41.7 9.7 %while.41 = (s32[]{:T(128)}, f32[4,128,4,64]{1,3,2,0:T(8,128)S(1)}, f32[4,4,128]{2,1,0:T(4,128)S(1)}, f32[4,4,128,384]{3,2,1,0:T(8,128)}, bf16[4,384,4,64]{1,3,2...) while((s32[]{:T(128)}, f32[4,128,4,64]{1,3,2,0:T(8,128)S(1)}, ...), condition=%wide.region_3.4_spmd.clone, body=%wide.region_0.3_spmd.sunk.clone | while | flops 52985344 | bytes 4892413 | solution.py:87
  51.5 2.6 %fusion.62 = f32[1024,1024]{1,0:T(8,128)} fusion(bf16[128,1024]{0,1:T(8,128)(2,1)S(1)} %bitcast.267, bf16[1,128,1024]{2,1,0:T(8,128)(2,1)S(1)} %copy-done), kind=kOutput, calls=%fused_computation.97 | convolution fusion | flops 268435456 | bytes 4718592 | tf_op jit(solution)/shard_map/dot_general | solution.py:174
  55.1 1.5 collective-permute-start.8
  59.3 4.5 %collective-permute-start.10 = (f32[128,16]{0,1:T(8,128)S(1)}, f32[128,16]{0,1:T(8,128)S(1)}, u32[]{:S(2)}, u32[]{:S(2)}) collective-permute-start(f32[128,16]{0,1:T(8,128)S(1)} %bitcast.295), channel_id=1, source_target_pairs={{0,16},{1,17},{2,18},{3,19},{4,20},{5,21},{6,22},{7,23},{8,24},{9,... | collective-permute-start | bytes 24584 | tf_op jit(solution)/shard_map/ppermute | solution.py:15
  66.7 2.7 %collective-permute-done.11 = f32[128,16]{0,1:T(8,128)S(1)} collective-permute-done((f32[128,16]{0,1:T(8,128)S(1)}, f32[128,16]{0,1:T(8,128)S(1)}, u32[]{:S(2)}, u32[]{:S(2)}) %collective-permute-start.11) | collective-permute-done | bytes 8224 | tf_op jit(solution)/shard_map/ppermute | solution.py:15
  69.4 3.1 %convert_multiply_fusion = (f32[128,1024]{1,0:T(8,128)S(1)}, bf16[128,1024]{1,0:T(8,128)(2,1)}) fusion(f32[128,1024]{1,0:T(8,128)S(1)} %copy.39, bf16[1024,1024]{1,0:T(8,128)(2,1)} %all-gather.2.cloned.1.call-done, bf16[1,128,1024]{2,1,0:T(8,128)(2,1)S(1)} %copy-done), kind=kOutput, calls=%fused_computation.96 | convolution fusion | flops 268828672 | bytes 3670016 | tf_op jit(solution)/shard_map/dot_general | solution.py:60
  73.4 1.9 %collective-permute-start.14 = (f32[128,16]{0,1:T(8,128)}, f32[128,16]{0,1:T(8,128)S(1)}, u32[]{:S(2)}, u32[]{:S(2)}) collective-permute-start(f32[128,16]{0,1:T(8,128)} %bitcast_reduce_fusion), channel_id=1, source_target_pairs={{0,16},{1,17},{2,18},{3,19},{4,20},{5,21},{6,22},{7,23},{8,24},{9,... | collective-permute-start | bytes 24584 | tf_op jit(solution)/shard_map/ppermute | solution.py:15
  76.6 5.3 %collective-permute-start.12 = (bf16[128,1024]{1,0:T(8,128)(2,1)}, bf16[128,1024]{1,0:T(8,128)(2,1)}, u32[]{:S(2)}, u32[]{:S(2)}) collective-permute-start(bf16[128,1024]{1,0:T(8,128)(2,1)} %get-tuple-element.364), channel_id=1, source_target_pairs={{0,16},{1,17},{2,18},{3,19},{4,20},{5,21},{6,22},{7,23},{8,24},{9,... | collective-permute-start | bytes 786440 | tf_op jit(solution)/shard_map/ppermute | solution.py:15
  83.1 1.8 %copy.38 = bf16[128,1024]{0,1:T(8,128)(2,1)} copy(bf16[128,1024]{1,0:T(8,128)(2,1)} %get-tuple-element.364) | data formatting | bytes 524288 | tf_op jit(solution)/shard_map/convert_element_type | solution.py:62
  84.9 15.8 %while.42 = (s32[]{:T(128)}, bf16[4,128,4,64]{1,3,2,0:T(8,128)(2,1)S(1)}, f32[4,2,4]{2,1,0:T(2,128)S(1)}, bf16[4,384,4,64]{1,3,2,0:T(8,128)(2,1)}, f32[4,4,128,3...) while((s32[]{:T(128)}, ...), condition=%wide.region_8.9_spmd.clone, body=%wide.region_5.8_spmd.sunk.clone | while | flops 51789824 | bytes 2273933 | solution.py:121
  85.9 1.8 %select_reduce_fusion.8 = (f32[4]{0:T(128)S(1)}, f32[4]{0:T(128)S(1)}, bf16[4,128,384]{2,1,0:T(8,128)(2,1)S(1)}) fusion(pred[128,384]{1,0:T(8,128)(4,1)S(1)} %broadcast_compare_fusion.12, f32[4,128]{1,0:T(4,128)S(1)} %dynamic-slice_bitcast_fusion.7, bf16[4,384,4,64]{1,3,2,0:T(8,128)(2,1)} %get-tuple-element.778, s32[]{:T(128)} %get-tuple-element.762, ...), kind=kOutput, calls=%fused_computation.34.clone.1.clone | convolution fusion | flops 26542072 | bytes 1494560 | tf_op jit(solution)/shard_map/while/body/eval_jaxpr/qhd,khd->hqk/dot_general | solution.py:102
  89.8 1.8 %select_reduce_fusion.8 = (f32[4]{0:T(128)S(1)}, f32[4]{0:T(128)S(1)}, bf16[4,128,384]{2,1,0:T(8,128)(2,1)S(1)}) fusion(pred[128,384]{1,0:T(8,128)(4,1)S(1)} %broadcast_compare_fusion.12, f32[4,128]{1,0:T(4,128)S(1)} %dynamic-slice_bitcast_fusion.7, bf16[4,384,4,64]{1,3,2,0:T(8,128)(2,1)} %get-tuple-element.778, s32[]{:T(128)} %get-tuple-element.762, ...), kind=kOutput, calls=%fused_computation.34.clone.1.clone | convolution fusion | flops 26542072 | bytes 1494560 | tf_op jit(solution)/shard_map/while/body/eval_jaxpr/qhd,khd->hqk/dot_general | solution.py:102
  93.6 1.8 select_reduce_fusion.8
  97.4 2.0 %select_reduce_fusion.8 = (f32[4]{0:T(128)S(1)}, f32[4]{0:T(128)S(1)}, bf16[4,128,384]{2,1,0:T(8,128)(2,1)S(1)}) fusion(pred[128,384]{1,0:T(8,128)(4,1)S(1)} %broadcast_compare_fusion.12, f32[4,128]{1,0:T(4,128)S(1)} %dynamic-slice_bitcast_fusion.7, bf16[4,384,4,64]{1,3,2,0:T(8,128)(2,1)} %get-tuple-element.778, s32[]{:T(128)} %get-tuple-element.762, ...), kind=kOutput, calls=%fused_computation.34.clone.1.clone | convolution fusion | flops 26542072 | bytes 1494560 | tf_op jit(solution)/shard_map/while/body/eval_jaxpr/qhd,khd->hqk/dot_general | solution.py:102
  102.0 42.5 %psum.15 = f32[2,16]{1,0:T(2,128)} all-reduce(f32[2,16]{1,0:T(2,128)S(1)} %reshape.290), channel_id=1, replica_groups=mesh['ctx'=2,'dp'=16] {'ctx','dp'}, use_global_device_ids=true, to_apply=%region_13.14 | all-reduce | flops 32 | bytes 256 | tf_op jit(solution)/shard_map/psum | solution.py:182
  147.7 12.6 %while.43 = (s32[]{:T(128)}, bf16[4,128,4,64]{1,3,2,0:T(8,128)(2,1)S(1)}, bf16[4,128,4,64]{1,3,2,0:T(8,128)(2,1)}, bf16[4,384,4,64]{1,3,2,0:T(8,128)(2,1)S(1)}, ...) while((s32[]{:T(128)}, ...), condition=%wide.region_10.11_spmd.clone, body=%wide.region_9.10_spmd.sunk.clone | while | flops 102760448 | bytes 4109073 | solution.py:157
  161.2 1.8 copy.49
  163.0 8.4 %all-reduce.2.cloned.1.call-done = f32[64,1024]{1,0:T(8,128)} async-done(((f32[64,1024]{1,0:T(8,128)}), f32[64,1024]{1,0:T(8,128)}) %all-reduce.2.cloned.1.call-update) | async-done | bytes 262160 | tf_op jit(solution)/shard_map/psum | solution.py:181
  171.4 1.7 copy.100
  (176 shorter events, 61.0 us)
Async XLA Ops:
  7.2 44.3 %copy-start = (bf16[1,128,1024]{2,1,0:T(8,128)(2,1)S(1)}, bf16[1,128,1024]{2,1,0:T(8,128)(2,1)}, u32[]{:S(2)}) copy-start(bf16[1,128,1024]{2,1,0:T(8,128)(2,1)} %param.17) | copy-start | bytes 786436
  7.2 24.3 %copy-start.7 = (bf16[1,128,1024]{2,1,0:T(8,128)(2,1)S(1)}, bf16[1,128,1024]{2,1,0:T(8,128)(2,1)}, u32[]{:S(2)}) copy-start(bf16[1,128,1024]{2,1,0:T(8,128)(2,1)} %param.15) | copy-start | bytes 786436
  7.2 23.0 %copy-start.11 = (s32[1,128]{1,0:T(1,128)S(1)}, s32[1,128]{1,0:T(1,128)}, u32[]{:S(2)}) copy-start(s32[1,128]{1,0:T(1,128)} %param.19) | copy-start | bytes 1540
  7.2 22.9 %copy-start.12 = (f32[2,16]{1,0:T(2,128)S(1)}, f32[2,16]{1,0:T(2,128)}, u32[]{:S(2)}) copy-start(f32[2,16]{1,0:T(2,128)} %param.20) | copy-start | bytes 388
  7.2 62.2 %all-gather.2.cloned.1.call-start = ((), (), s32[]{:S(2)}) async-start(), calls=%async_computation.1 | async-start | bytes 2228224 | tf_op jit(solution)/shard_map/all_gather | solution.py:59
  8.4 27.4 %collective-permute-start = (bf16[128,1024]{0,1:T(8,128)(2,1)S(1)}, bf16[128,1024]{0,1:T(8,128)(2,1)S(1)}, u32[]{:S(2)}, u32[]{:S(2)}) collective-permute-start(bf16[128,1024]{0,1:T(8,128)(2,1)S(1)} %bitcast.263), channel_id=1, source_target_pairs={{0,16},{1,17},{2,18},{3,19},{4,20},{5,21},{6,22},{7,23},{8,24},{9,... | collective-permute-start | bytes 786440 | tf_op jit(solution)/shard_map/ppermute | solution.py:15
  13.4 22.5 %collective-permute-start.1 = (bf16[128,1024]{0,1:T(8,128)(2,1)S(1)}, bf16[128,1024]{0,1:T(8,128)(2,1)S(1)}, u32[]{:S(2)}, u32[]{:S(2)}) collective-permute-start(bf16[128,1024]{0,1:T(8,128)(2,1)S(1)} %bitcast.264), channel_id=1, source_target_pairs={{16,0},{17,1},{18,2},{19,3},{20,4},{21,5},{22,6},{23,7},{24,8},{25... | collective-permute-start | bytes 786440 | tf_op jit(solution)/shard_map/ppermute | solution.py:15
  14.7 21.0 %collective-permute-start.4 = (bf16[128,1024]{1,0:T(8,128)(2,1)}, bf16[128,1024]{1,0:T(8,128)(2,1)S(1)}, u32[]{:S(2)}, u32[]{:S(2)}) collective-permute-start(bf16[128,1024]{1,0:T(8,128)(2,1)} %bitcast.278), channel_id=1, source_target_pairs={{0,16},{1,17},{2,18},{3,19},{4,20},{5,21},{6,22},{7,23},{8,24},{9,... | collective-permute-start | bytes 786440 | tf_op jit(solution)/shard_map/ppermute | solution.py:15
  19.9 4.7 %collective-permute-start.2 = (s32[128]{0:T(128)S(1)}, s32[128]{0:T(128)S(1)}, u32[]{:S(2)}, u32[]{:S(2)}) collective-permute-start(s32[128]{0:T(128)S(1)} %add_bitcast_fusion), channel_id=1, source_target_pairs={{0,16},{1,17},{2,18},{3,19},{4,20},{5,21},{6,22},{7,23},{8,24},{9,... | collective-permute-start | bytes 1544 | tf_op jit(solution)/shard_map/ppermute | solution.py:15
  21.2 9.0 %collective-permute-start.3 = (s32[128]{0:T(128)S(1)}, s32[128]{0:T(128)S(1)}, u32[]{:S(2)}, u32[]{:S(2)}) collective-permute-start(s32[128]{0:T(128)S(1)} %add_bitcast_fusion), channel_id=1, source_target_pairs={{16,0},{17,1},{18,2},{19,3},{20,4},{21,5},{22,6},{23,7},{24,8},{25... | collective-permute-start | bytes 1544 | tf_op jit(solution)/shard_map/ppermute | solution.py:15
  22.5 125.2 %reduce-scatter.2.cloned.1.call-start = ((), (), s32[]{:S(2)}) async-start(), calls=%async_computation.2 | async-start | bytes 4456448 | tf_op jit(solution)/shard_map/reduce_scatter | solution.py:173
  23.7 17.0 %copy-start.6 = (bf16[1,128,1024]{1,2,0:T(8,128)(2,1)}, bf16[1,128,1024]{1,2,0:T(8,128)(2,1)S(1)}, u32[]{:S(2)}) copy-start(bf16[1,128,1024]{1,2,0:T(8,128)(2,1)S(1)} %copy.34) | copy-start | bytes 786436
  24.6 6.9 %collective-permute-start.6 = (s32[128]{0:T(128)}, s32[128]{0:T(128)S(1)}, u32[]{:S(2)}, u32[]{:S(2)}) collective-permute-start(s32[128]{0:T(128)} %bitcast.285), channel_id=1, source_target_pairs={{0,16},{1,17},{2,18},{3,19},{4,20},{5,21},{6,22},{7,23},{8,24},{9,... | collective-permute-start | bytes 1544 | tf_op jit(solution)/shard_map/ppermute | solution.py:15
  30.2 5.5 %collective-permute-start.7 = (s32[128]{0:T(128)S(1)}, s32[128]{0:T(128)S(1)}, u32[]{:S(2)}, u32[]{:S(2)}) collective-permute-start(s32[128]{0:T(128)S(1)} %bitcast.286), channel_id=1, source_target_pairs={{16,0},{17,1},{18,2},{19,3},{20,4},{21,5},{22,6},{23,7},{24,8},{25... | collective-permute-start | bytes 1544 | tf_op jit(solution)/shard_map/ppermute | solution.py:15
  31.5 8.3 %collective-permute-start.5 = (bf16[128,1024]{1,0:T(8,128)(2,1)S(1)}, bf16[128,1024]{1,0:T(8,128)(2,1)S(1)}, u32[]{:S(2)}, u32[]{:S(2)}) collective-permute-start(bf16[128,1024]{1,0:T(8,128)(2,1)S(1)} %bitcast.279), channel_id=1, source_target_pairs={{16,0},{17,1},{18,2},{19,3},{20,4},{21,5},{22,6},{23,7},{24,8},{25... | collective-permute-start | bytes 786440 | tf_op jit(solution)/shard_map/ppermute | solution.py:15
  54.1 117.2 %all-reduce.2.cloned.1.call-start = ((), (), s32[]{:S(2)}) async-start(), calls=%async_computation.3 | async-start | bytes 524288 | tf_op jit(solution)/shard_map/psum | solution.py:181
  55.1 10.1 %collective-permute-start.8 = (bf16[128,1024]{1,0:T(8,128)(2,1)S(1)}, bf16[128,1024]{1,0:T(8,128)(2,1)S(1)}, u32[]{:S(2)}, u32[]{:S(2)}) collective-permute-start(bf16[128,1024]{1,0:T(8,128)(2,1)S(1)} %bitcast.280), channel_id=1, source_target_pairs={{0,16},{1,17},{2,18},{3,19},{4,20},{5,21},{6,22},{7,23},{8,24},{9,... | collective-permute-start | bytes 786440 | tf_op jit(solution)/shard_map/ppermute | solution.py:15
  56.5 8.8 %collective-permute-start.9 = (bf16[128,1024]{1,0:T(8,128)(2,1)S(1)}, bf16[128,1024]{1,0:T(8,128)(2,1)S(1)}, u32[]{:S(2)}, u32[]{:S(2)}) collective-permute-start(bf16[128,1024]{1,0:T(8,128)(2,1)S(1)} %bitcast.281), channel_id=1, source_target_pairs={{16,0},{17,1},{18,2},{19,3},{20,4},{21,5},{22,6},{23,7},{24,8},{25... | collective-permute-start | bytes 786440 | tf_op jit(solution)/shard_map/ppermute | solution.py:15
  59.3 7.4 %collective-permute-start.10 = (f32[128,16]{0,1:T(8,128)S(1)}, f32[128,16]{0,1:T(8,128)S(1)}, u32[]{:S(2)}, u32[]{:S(2)}) collective-permute-start(f32[128,16]{0,1:T(8,128)S(1)} %bitcast.295), channel_id=1, source_target_pairs={{0,16},{1,17},{2,18},{3,19},{4,20},{5,21},{6,22},{7,23},{8,24},{9,... | collective-permute-start | bytes 24584 | tf_op jit(solution)/shard_map/ppermute | solution.py:15
  63.8 5.5 %collective-permute-start.11 = (f32[128,16]{0,1:T(8,128)S(1)}, f32[128,16]{0,1:T(8,128)S(1)}, u32[]{:S(2)}, u32[]{:S(2)}) collective-permute-start(f32[128,16]{0,1:T(8,128)S(1)} %bitcast.296), channel_id=1, source_target_pairs={{16,0},{17,1},{18,2},{19,3},{20,4},{21,5},{22,6},{23,7},{24,8},{25... | collective-permute-start | bytes 24584 | tf_op jit(solution)/shard_map/ppermute | solution.py:15
  73.4 71.9 %collective-permute-start.14 = (f32[128,16]{0,1:T(8,128)}, f32[128,16]{0,1:T(8,128)S(1)}, u32[]{:S(2)}, u32[]{:S(2)}) collective-permute-start(f32[128,16]{0,1:T(8,128)} %bitcast_reduce_fusion), channel_id=1, source_target_pairs={{0,16},{1,17},{2,18},{3,19},{4,20},{5,21},{6,22},{7,23},{8,24},{9,... | collective-permute-start | bytes 24584 | tf_op jit(solution)/shard_map/ppermute | solution.py:15
  75.3 70.0 %collective-permute-start.15 = (f32[128,16]{0,1:T(8,128)}, f32[128,16]{0,1:T(8,128)S(1)}, u32[]{:S(2)}, u32[]{:S(2)}) collective-permute-start(f32[128,16]{0,1:T(8,128)} %bitcast_reduce_fusion), channel_id=1, source_target_pairs={{16,0},{17,1},{18,2},{19,3},{20,4},{21,5},{22,6},{23,7},{24,8},{25... | collective-permute-start | bytes 24584 | tf_op jit(solution)/shard_map/ppermute | solution.py:15
  76.6 69.5 %collective-permute-start.12 = (bf16[128,1024]{1,0:T(8,128)(2,1)}, bf16[128,1024]{1,0:T(8,128)(2,1)}, u32[]{:S(2)}, u32[]{:S(2)}) collective-permute-start(bf16[128,1024]{1,0:T(8,128)(2,1)} %get-tuple-element.364), channel_id=1, source_target_pairs={{0,16},{1,17},{2,18},{3,19},{4,20},{5,21},{6,22},{7,23},{8,24},{9,... | collective-permute-start | bytes 786440 | tf_op jit(solution)/shard_map/ppermute | solution.py:15
  81.8 64.2 %collective-permute-start.13 = (bf16[128,1024]{1,0:T(8,128)(2,1)}, bf16[128,1024]{1,0:T(8,128)(2,1)}, u32[]{:S(2)}, u32[]{:S(2)}) collective-permute-start(bf16[128,1024]{1,0:T(8,128)(2,1)} %get-tuple-element.364), channel_id=1, source_target_pairs={{16,0},{17,1},{18,2},{19,3},{20,4},{21,5},{22,6},{23,7},{24,8},{25... | collective-permute-start | bytes 786440 | tf_op jit(solution)/shard_map/ppermute | solution.py:15
  (8 other events, 27.1 us)
Sparse Core Ops, SparseCore 0:
  22.6 43.8 all-gather.1
  70.4 72.1 reduce-scatter.1
  147.8 23.4 all-reduce.1
where the time goes:
time: 181 us; the launch traced here: 180 us
  blocking collectives  42.5 us (23%)
  starting transfers between devices  38.7 us (21%)
  matrix products  33.7 us (19%)
  local copies, waits for them, and re-layouts  19.3 us (11%)
  waiting for transfers between devices  16.9 us (9%)
  between operations  14.2 us (8%)
  other arithmetic  13.7 us (8%)
    psum x1, blocking collectives, on_device(): bias_grad = lax.psum(bias_terms, ('ctx', 'dp'))  42.5 us
    ppermute x16, starting transfers between devices, shifted_2(): return lax.ppermute(shard, axis, pairs)  38.6 us
    unnamed x35, local copies, waits for them, and re-layouts  11.7 us
    psum x1, waiting for transfers between devices, on_device(): w_grad = lax.psum(partial_rows, 'ctx')  8.41 us
    ppermute x16, waiting for transfers between devices, shifted_2(): return lax.ppermute(shard, axis, pairs)  8.41 us
    dot_general x4, matrix products, query_group(): jnp.einsum('qhd,khd->hqk', d_group, v_group, preferred_element_type=jnp.f...  7.44 us
    dot_general x8, matrix products, scored(): jnp.einsum('qhd,khd->hqk', q_group, k_group, preferred_element_type=jnp.f...  7.35 us
    dot_general x4, matrix products, query_group(): jnp.einsum('hqk,khd->qhd', dscore.astype(jnp.bfloat16), k_group, preferre...  4.94 us
  transfers between devices with their start and end apart: 19, of which 5 were waited for; matrix products, arithmetic and copies ran while one was open for 35% of the time, Pallas kernels for 0%

commit v1 on v0

--- a/solution.py
+++ b/solution.py
@@ -179,7 +179,7 @@
         tiled=True,
     )
     w_grad = lax.psum(partial_rows, "ctx")
-    bias_grad = lax.psum(bias_terms, ("ctx", "dp"))
+    bias_grad = jnp.sum(lax.all_gather(bias_terms, ("ctx", "dp")), axis=0)
     return (mixed[None], q_out[None], k_out[None], v_out[None], w_grad, bias_grad)
 
 

time: 181 us -> 179 us (0.989)
  waiting for transfers between devices: 16.9 us -> 13.4 us
    all_gather x0 -> x1, blocking collectives: none -> 43.7 us  [on_device(): bias_grad = jnp.sum(lax.all_gather(bias_terms, ('ctx', 'dp')), axis=0)]
    psum x1 -> x0, blocking collectives: 42.5 us -> none  [on_device(): bias_grad = lax.psum(bias_terms, ('ctx', 'dp'))]
    psum x1, waiting for transfers between devices: 8.41 us -> 4.89 us  [on_device(): w_grad = lax.psum(partial_rows, 'ctx')]
where the time goes in v1:
time: 179 us; the launch traced here: 177 us
  blocking collectives  43.7 us (24%)
  starting transfers between devices  38.7 us (22%)
  matrix products  33.7 us (19%)
  local copies, waits for them, and re-layouts  18.7 us (10%)
  other arithmetic  14.4 us (8%)
  between operations  14.2 us (8%)
  waiting for transfers between devices  13.4 us (7%)
    all_gather x1, blocking collectives, on_device(): bias_grad = jnp.sum(lax.all_gather(bias_terms, ('ctx', 'dp')), axis=0)  43.7 us
    ppermute x16, starting transfers between devices, shifted_2(): return lax.ppermute(shard, axis, pairs)  38.6 us
    unnamed x35, local copies, waits for them, and re-layouts  11.7 us
    ppermute x16, waiting for transfers between devices, shifted_2(): return lax.ppermute(shard, axis, pairs)  8.41 us
    dot_general x4, matrix products, query_group(): jnp.einsum('qhd,khd->hqk', d_group, v_group, preferred_element_type=jnp.f...  7.44 us
    dot_general x8, matrix products, scored(): jnp.einsum('qhd,khd->hqk', q_group, k_group, preferred_element_type=jnp.f...  7.36 us
    dot_general x4, matrix products, query_group(): jnp.einsum('hqk,khd->qhd', dscore.astype(jnp.bfloat16), k_group, preferre...  4.94 us
    psum x1, waiting for transfers between devices, on_device(): w_grad = lax.psum(partial_rows, 'ctx')  4.89 us
  transfers between devices with their start and end apart: 19, of which 5 were waited for; matrix products, arithmetic and copies ran while one was open for 35% of the time, Pallas kernels for 0%

profile of v1, /device:TPU:0, one launch (start us, length us, event | category | flops | bytes accessed | tf_op | source)
XLA Modules:
  0.0 177.3 jit_solution(12168976539316292407)
XLA Ops:
  8.4 4.9 %collective-permute-start = (bf16[128,1024]{0,1:T(8,128)(2,1)S(1)}, bf16[128,1024]{0,1:T(8,128)(2,1)S(1)}, u32[]{:S(2)}, u32[]{:S(2)}) collective-permute-start(bf16[128,1024]{0,1:T(8,128)(2,1)S(1)} %bitcast.265), channel_id=1, source_target_pairs={{0,16},{1,17},{2,18},{3,19},{4,20},{5,21},{6,22},{7,23},{8,24},{9,... | collective-permute-start | bytes 786440 | tf_op jit(solution)/shard_map/ppermute | solution.py:15
  14.7 4.6 %collective-permute-start.4 = (bf16[128,1024]{1,0:T(8,128)(2,1)}, bf16[128,1024]{1,0:T(8,128)(2,1)S(1)}, u32[]{:S(2)}, u32[]{:S(2)}) collective-permute-start(bf16[128,1024]{1,0:T(8,128)(2,1)} %bitcast.279), channel_id=1, source_target_pairs={{0,16},{1,17},{2,18},{3,19},{4,20},{5,21},{6,22},{7,23},{8,24},{9,... | collective-permute-start | bytes 786440 | tf_op jit(solution)/shard_map/ppermute | solution.py:15
  24.6 4.4 %collective-permute-start.6 = (s32[128]{0:T(128)}, s32[128]{0:T(128)S(1)}, u32[]{:S(2)}, u32[]{:S(2)}) collective-permute-start(s32[128]{0:T(128)} %bitcast.286), channel_id=1, source_target_pairs={{0,16},{1,17},{2,18},{3,19},{4,20},{5,21},{6,22},{7,23},{8,24},{9,... | collective-permute-start | bytes 1544 | tf_op jit(solution)/shard_map/ppermute | solution.py:15
  32.8 2.8 %collective-permute-done.7 = s32[128]{0:T(128)S(1)} collective-permute-done((s32[128]{0:T(128)S(1)}, s32[128]{0:T(128)S(1)}, u32[]{:S(2)}, u32[]{:S(2)}) %collective-permute-start.7) | collective-permute-done | bytes 544 | tf_op jit(solution)/shard_map/ppermute | solution.py:15
  37.8 2.0 %collective-permute-done.5 = bf16[128,1024]{1,0:T(8,128)(2,1)S(1)} collective-permute-done((bf16[128,1024]{1,0:T(8,128)(2,1)S(1)}, bf16[128,1024]{1,0:T(8,128)(2,1)S(1)}, u32[]{:S(2)}, u32[]{:S(2)}) %collective-permute-start.5) | collective-permute-done | bytes 262176 | tf_op jit(solution)/shard_map/ppermute | solution.py:15
  41.7 9.7 %while.41 = (s32[]{:T(128)}, f32[4,128,4,64]{1,3,2,0:T(8,128)S(1)}, f32[4,4,128]{2,1,0:T(4,128)S(1)}, f32[4,4,128,384]{3,2,1,0:T(8,128)}, bf16[4,384,4,64]{1,3,2...) while((s32[]{:T(128)}, f32[4,128,4,64]{1,3,2,0:T(8,128)S(1)}, ...), condition=%wide.region_3.4_spmd.clone, body=%wide.region_0.3_spmd.sunk.clone | while | flops 52985344 | bytes 4892413 | solution.py:87
  51.5 2.6 %fusion.64 = f32[1024,1024]{1,0:T(8,128)} fusion(bf16[128,1024]{0,1:T(8,128)(2,1)S(1)} %bitcast.269, bf16[1,128,1024]{2,1,0:T(8,128)(2,1)S(1)} %copy-done), kind=kOutput, calls=%fused_computation.97 | convolution fusion | flops 268435456 | bytes 4718592 | tf_op jit(solution)/shard_map/dot_general | solution.py:174
  55.1 1.5 collective-permute-start.8
  59.3 4.5 %collective-permute-start.10 = (f32[128,16]{0,1:T(8,128)S(1)}, f32[128,16]{0,1:T(8,128)S(1)}, u32[]{:S(2)}, u32[]{:S(2)}) collective-permute-start(f32[128,16]{0,1:T(8,128)S(1)} %bitcast.296), channel_id=1, source_target_pairs={{0,16},{1,17},{2,18},{3,19},{4,20},{5,21},{6,22},{7,23},{8,24},{9,... | collective-permute-start | bytes 24584 | tf_op jit(solution)/shard_map/ppermute | solution.py:15
  66.7 2.7 %collective-permute-done.11 = f32[128,16]{0,1:T(8,128)S(1)} collective-permute-done((f32[128,16]{0,1:T(8,128)S(1)}, f32[128,16]{0,1:T(8,128)S(1)}, u32[]{:S(2)}, u32[]{:S(2)}) %collective-permute-start.11) | collective-permute-done | bytes 8224 | tf_op jit(solution)/shard_map/ppermute | solution.py:15
  69.4 3.1 %convert_multiply_fusion = (f32[128,1024]{1,0:T(8,128)S(1)}, bf16[128,1024]{1,0:T(8,128)(2,1)}) fusion(f32[128,1024]{1,0:T(8,128)S(1)} %copy.58, bf16[1024,1024]{1,0:T(8,128)(2,1)} %all-gather.2.cloned.1.call-done, bf16[1,128,1024]{2,1,0:T(8,128)(2,1)S(1)} %copy-done), kind=kOutput, calls=%fused_computation.96 | convolution fusion | flops 268828672 | bytes 3670016 | tf_op jit(solution)/shard_map/dot_general | solution.py:60
  73.4 1.9 %collective-permute-start.14 = (f32[128,16]{0,1:T(8,128)}, f32[128,16]{0,1:T(8,128)S(1)}, u32[]{:S(2)}, u32[]{:S(2)}) collective-permute-start(f32[128,16]{0,1:T(8,128)} %bitcast_reduce_fusion), channel_id=1, source_target_pairs={{0,16},{1,17},{2,18},{3,19},{4,20},{5,21},{6,22},{7,23},{8,24},{9,... | collective-permute-start | bytes 24584 | tf_op jit(solution)/shard_map/ppermute | solution.py:15
  76.6 5.3 %collective-permute-start.12 = (bf16[128,1024]{1,0:T(8,128)(2,1)}, bf16[128,1024]{1,0:T(8,128)(2,1)}, u32[]{:S(2)}, u32[]{:S(2)}) collective-permute-start(bf16[128,1024]{1,0:T(8,128)(2,1)} %get-tuple-element.396), channel_id=1, source_target_pairs={{0,16},{1,17},{2,18},{3,19},{4,20},{5,21},{6,22},{7,23},{8,24},{9,... | collective-permute-start | bytes 786440 | tf_op jit(solution)/shard_map/ppermute | solution.py:15
  83.1 1.8 %copy.57 = bf16[128,1024]{0,1:T(8,128)(2,1)} copy(bf16[128,1024]{1,0:T(8,128)(2,1)} %get-tuple-element.396) | data formatting | bytes 524288 | tf_op jit(solution)/shard_map/convert_element_type | solution.py:62
  84.9 15.8 %while.42 = (s32[]{:T(128)}, bf16[4,128,4,64]{1,3,2,0:T(8,128)(2,1)S(1)}, f32[4,2,4]{2,1,0:T(2,128)S(1)}, bf16[4,384,4,64]{1,3,2,0:T(8,128)(2,1)}, f32[4,4,128,3...) while((s32[]{:T(128)}, ...), condition=%wide.region_8.9_spmd.clone, body=%wide.region_5.8_spmd.sunk.clone | while | flops 51789824 | bytes 2273933 | solution.py:121
  85.9 1.8 %select_reduce_fusion.8 = (f32[4]{0:T(128)S(1)}, f32[4]{0:T(128)S(1)}, bf16[4,128,384]{2,1,0:T(8,128)(2,1)S(1)}) fusion(pred[128,384]{1,0:T(8,128)(4,1)S(1)} %broadcast_compare_fusion.12, f32[4,128]{1,0:T(4,128)S(1)} %dynamic-slice_bitcast_fusion.7, bf16[4,384,4,64]{1,3,2,0:T(8,128)(2,1)} %get-tuple-element.810, s32[]{:T(128)} %get-tuple-element.794, ...), kind=kOutput, calls=%fused_computation.34.clone.1.clone | convolution fusion | flops 26542072 | bytes 1494560 | tf_op jit(solution)/shard_map/while/body/eval_jaxpr/qhd,khd->hqk/dot_general | solution.py:102
  89.8 1.8 %select_reduce_fusion.8 = (f32[4]{0:T(128)S(1)}, f32[4]{0:T(128)S(1)}, bf16[4,128,384]{2,1,0:T(8,128)(2,1)S(1)}) fusion(pred[128,384]{1,0:T(8,128)(4,1)S(1)} %broadcast_compare_fusion.12, f32[4,128]{1,0:T(4,128)S(1)} %dynamic-slice_bitcast_fusion.7, bf16[4,384,4,64]{1,3,2,0:T(8,128)(2,1)} %get-tuple-element.810, s32[]{:T(128)} %get-tuple-element.794, ...), kind=kOutput, calls=%fused_computation.34.clone.1.clone | convolution fusion | flops 26542072 | bytes 1494560 | tf_op jit(solution)/shard_map/while/body/eval_jaxpr/qhd,khd->hqk/dot_general | solution.py:102
  93.6 1.8 %select_reduce_fusion.8 = (f32[4]{0:T(128)S(1)}, f32[4]{0:T(128)S(1)}, bf16[4,128,384]{2,1,0:T(8,128)(2,1)S(1)}) fusion(pred[128,384]{1,0:T(8,128)(4,1)S(1)} %broadcast_compare_fusion.12, f32[4,128]{1,0:T(4,128)S(1)} %dynamic-slice_bitcast_fusion.7, bf16[4,384,4,64]{1,3,2,0:T(8,128)(2,1)} %get-tuple-element.810, s32[]{:T(128)} %get-tuple-element.794, ...), kind=kOutput, calls=%fused_computation.34.clone.1.clone | convolution fusion | flops 26542072 | bytes 1494560 | tf_op jit(solution)/shard_map/while/body/eval_jaxpr/qhd,khd->hqk/dot_general | solution.py:102
  97.4 2.0 %select_reduce_fusion.8 = (f32[4]{0:T(128)S(1)}, f32[4]{0:T(128)S(1)}, bf16[4,128,384]{2,1,0:T(8,128)(2,1)S(1)}) fusion(pred[128,384]{1,0:T(8,128)(4,1)S(1)} %broadcast_compare_fusion.12, f32[4,128]{1,0:T(4,128)S(1)} %dynamic-slice_bitcast_fusion.7, bf16[4,384,4,64]{1,3,2,0:T(8,128)(2,1)} %get-tuple-element.810, s32[]{:T(128)} %get-tuple-element.794, ...), kind=kOutput, calls=%fused_computation.34.clone.1.clone | convolution fusion | flops 26542072 | bytes 1494560 | tf_op jit(solution)/shard_map/while/body/eval_jaxpr/qhd,khd->hqk/dot_general | solution.py:102
  102.8 43.7 %all_gather.7 = f32[32,2,16]{2,1,0:T(2,128)S(1)} all-gather(f32[1,2,16]{2,1,0:T(2,128)S(1)} %all_gather_reshape.3), channel_id=1, replica_groups=mesh['ctx'=2,'dp'=16] {'ctx','dp'}, dimensions={0}, use_global_device_ids=true | all-gather | bytes 4224 | tf_op jit(solution)/shard_map/all_gather | solution.py:182
  149.6 12.0 %while.43 = (s32[]{:T(128)}, bf16[4,128,4,64]{1,3,2,0:T(8,128)(2,1)S(1)}, bf16[4,128,4,64]{1,3,2,0:T(8,128)(2,1)}, bf16[4,384,4,64]{1,3,2,0:T(8,128)(2,1)S(1)}, ...) while((s32[]{:T(128)}, ...), condition=%wide.region_10.11_spmd.clone, body=%wide.region_9.10_spmd.sunk.clone | while | flops 102760448 | bytes 3781901 | solution.py:157
  162.4 1.8 %copy.67 = bf16[1,128,1024]{2,1,0:T(8,128)(2,1)} copy(bf16[1,128,1024]{1,2,0:T(8,128)(2,1)} %bitcast.79) | data formatting | bytes 524288
  164.2 4.9 %all-reduce.2.cloned.1.call-done = f32[64,1024]{1,0:T(8,128)} async-done(((f32[64,1024]{1,0:T(8,128)}), f32[64,1024]{1,0:T(8,128)}) %all-reduce.2.cloned.1.call-update) | async-done | bytes 262160 | tf_op jit(solution)/shard_map/psum | solution.py:181
  169.1 1.7 copy.107
  (169 shorter events, 61.0 us)
Async XLA Ops:
  7.2 44.3 %copy-start = (bf16[1,128,1024]{2,1,0:T(8,128)(2,1)S(1)}, bf16[1,128,1024]{2,1,0:T(8,128)(2,1)}, u32[]{:S(2)}) copy-start(bf16[1,128,1024]{2,1,0:T(8,128)(2,1)} %param.17) | copy-start | bytes 786436
  7.2 24.3 %copy-start.7 = (bf16[1,128,1024]{2,1,0:T(8,128)(2,1)S(1)}, bf16[1,128,1024]{2,1,0:T(8,128)(2,1)}, u32[]{:S(2)}) copy-start(bf16[1,128,1024]{2,1,0:T(8,128)(2,1)} %param.15) | copy-start | bytes 786436
  7.2 23.0 %copy-start.11 = (s32[1,128]{1,0:T(1,128)S(1)}, s32[1,128]{1,0:T(1,128)}, u32[]{:S(2)}) copy-start(s32[1,128]{1,0:T(1,128)} %param.19) | copy-start | bytes 1540
  7.2 22.9 %copy-start.12 = (f32[2,16]{1,0:T(2,128)S(1)}, f32[2,16]{1,0:T(2,128)}, u32[]{:S(2)}) copy-start(f32[2,16]{1,0:T(2,128)} %param.20) | copy-start | bytes 388
  7.2 62.2 %all-gather.2.cloned.1.call-start = ((), (), s32[]{:S(2)}) async-start(), calls=%async_computation.1 | async-start | bytes 2228224 | tf_op jit(solution)/shard_map/all_gather | solution.py:59
  8.4 27.4 %collective-permute-start = (bf16[128,1024]{0,1:T(8,128)(2,1)S(1)}, bf16[128,1024]{0,1:T(8,128)(2,1)S(1)}, u32[]{:S(2)}, u32[]{:S(2)}) collective-permute-start(bf16[128,1024]{0,1:T(8,128)(2,1)S(1)} %bitcast.265), channel_id=1, source_target_pairs={{0,16},{1,17},{2,18},{3,19},{4,20},{5,21},{6,22},{7,23},{8,24},{9,... | collective-permute-start | bytes 786440 | tf_op jit(solution)/shard_map/ppermute | solution.py:15
  13.4 22.5 %collective-permute-start.1 = (bf16[128,1024]{0,1:T(8,128)(2,1)S(1)}, bf16[128,1024]{0,1:T(8,128)(2,1)S(1)}, u32[]{:S(2)}, u32[]{:S(2)}) collective-permute-start(bf16[128,1024]{0,1:T(8,128)(2,1)S(1)} %bitcast.266), channel_id=1, source_target_pairs={{16,0},{17,1},{18,2},{19,3},{20,4},{21,5},{22,6},{23,7},{24,8},{25... | collective-permute-start | bytes 786440 | tf_op jit(solution)/shard_map/ppermute | solution.py:15
  14.7 21.0 %collective-permute-start.4 = (bf16[128,1024]{1,0:T(8,128)(2,1)}, bf16[128,1024]{1,0:T(8,128)(2,1)S(1)}, u32[]{:S(2)}, u32[]{:S(2)}) collective-permute-start(bf16[128,1024]{1,0:T(8,128)(2,1)} %bitcast.279), channel_id=1, source_target_pairs={{0,16},{1,17},{2,18},{3,19},{4,20},{5,21},{6,22},{7,23},{8,24},{9,... | collective-permute-start | bytes 786440 | tf_op jit(solution)/shard_map/ppermute | solution.py:15
  19.9 4.7 %collective-permute-start.2 = (s32[128]{0:T(128)S(1)}, s32[128]{0:T(128)S(1)}, u32[]{:S(2)}, u32[]{:S(2)}) collective-permute-start(s32[128]{0:T(128)S(1)} %add_bitcast_fusion), channel_id=1, source_target_pairs={{0,16},{1,17},{2,18},{3,19},{4,20},{5,21},{6,22},{7,23},{8,24},{9,... | collective-permute-start | bytes 1544 | tf_op jit(solution)/shard_map/ppermute | solution.py:15
  21.2 9.0 %collective-permute-start.3 = (s32[128]{0:T(128)S(1)}, s32[128]{0:T(128)S(1)}, u32[]{:S(2)}, u32[]{:S(2)}) collective-permute-start(s32[128]{0:T(128)S(1)} %add_bitcast_fusion), channel_id=1, source_target_pairs={{16,0},{17,1},{18,2},{19,3},{20,4},{21,5},{22,6},{23,7},{24,8},{25... | collective-permute-start | bytes 1544 | tf_op jit(solution)/shard_map/ppermute | solution.py:15
  22.5 127.0 %reduce-scatter.2.cloned.1.call-start = ((), (), s32[]{:S(2)}) async-start(), calls=%async_computation.2 | async-start | bytes 4456448 | tf_op jit(solution)/shard_map/reduce_scatter | solution.py:173
  23.7 17.0 %copy-start.6 = (bf16[1,128,1024]{1,2,0:T(8,128)(2,1)}, bf16[1,128,1024]{1,2,0:T(8,128)(2,1)S(1)}, u32[]{:S(2)}) copy-start(bf16[1,128,1024]{1,2,0:T(8,128)(2,1)S(1)} %copy.53) | copy-start | bytes 786436
  24.6 6.9 %collective-permute-start.6 = (s32[128]{0:T(128)}, s32[128]{0:T(128)S(1)}, u32[]{:S(2)}, u32[]{:S(2)}) collective-permute-start(s32[128]{0:T(128)} %bitcast.286), channel_id=1, source_target_pairs={{0,16},{1,17},{2,18},{3,19},{4,20},{5,21},{6,22},{7,23},{8,24},{9,... | collective-permute-start | bytes 1544 | tf_op jit(solution)/shard_map/ppermute | solution.py:15
  30.2 5.5 %collective-permute-start.7 = (s32[128]{0:T(128)S(1)}, s32[128]{0:T(128)S(1)}, u32[]{:S(2)}, u32[]{:S(2)}) collective-permute-start(s32[128]{0:T(128)S(1)} %bitcast.287), channel_id=1, source_target_pairs={{16,0},{17,1},{18,2},{19,3},{20,4},{21,5},{22,6},{23,7},{24,8},{25... | collective-permute-start | bytes 1544 | tf_op jit(solution)/shard_map/ppermute | solution.py:15
  31.5 8.3 %collective-permute-start.5 = (bf16[128,1024]{1,0:T(8,128)(2,1)S(1)}, bf16[128,1024]{1,0:T(8,128)(2,1)S(1)}, u32[]{:S(2)}, u32[]{:S(2)}) collective-permute-start(bf16[128,1024]{1,0:T(8,128)(2,1)S(1)} %bitcast.280), channel_id=1, source_target_pairs={{16,0},{17,1},{18,2},{19,3},{20,4},{21,5},{22,6},{23,7},{24,8},{25... | collective-permute-start | bytes 786440 | tf_op jit(solution)/shard_map/ppermute | solution.py:15
  54.1 115.0 %all-reduce.2.cloned.1.call-start = ((), (), s32[]{:S(2)}) async-start(), calls=%async_computation.3 | async-start | bytes 524288 | tf_op jit(solution)/shard_map/psum | solution.py:181
  55.1 10.1 %collective-permute-start.8 = (bf16[128,1024]{1,0:T(8,128)(2,1)S(1)}, bf16[128,1024]{1,0:T(8,128)(2,1)S(1)}, u32[]{:S(2)}, u32[]{:S(2)}) collective-permute-start(bf16[128,1024]{1,0:T(8,128)(2,1)S(1)} %bitcast.281), channel_id=1, source_target_pairs={{0,16},{1,17},{2,18},{3,19},{4,20},{5,21},{6,22},{7,23},{8,24},{9,... | collective-permute-start | bytes 786440 | tf_op jit(solution)/shard_map/ppermute | solution.py:15
  56.5 8.8 %collective-permute-start.9 = (bf16[128,1024]{1,0:T(8,128)(2,1)S(1)}, bf16[128,1024]{1,0:T(8,128)(2,1)S(1)}, u32[]{:S(2)}, u32[]{:S(2)}) collective-permute-start(bf16[128,1024]{1,0:T(8,128)(2,1)S(1)} %bitcast.282), channel_id=1, source_target_pairs={{16,0},{17,1},{18,2},{19,3},{20,4},{21,5},{22,6},{23,7},{24,8},{25... | collective-permute-start | bytes 786440 | tf_op jit(solution)/shard_map/ppermute | solution.py:15
  59.3 7.4 %collective-permute-start.10 = (f32[128,16]{0,1:T(8,128)S(1)}, f32[128,16]{0,1:T(8,128)S(1)}, u32[]{:S(2)}, u32[]{:S(2)}) collective-permute-start(f32[128,16]{0,1:T(8,128)S(1)} %bitcast.296), channel_id=1, source_target_pairs={{0,16},{1,17},{2,18},{3,19},{4,20},{5,21},{6,22},{7,23},{8,24},{9,... | collective-permute-start | bytes 24584 | tf_op jit(solution)/shard_map/ppermute | solution.py:15
  63.8 5.5 %collective-permute-start.11 = (f32[128,16]{0,1:T(8,128)S(1)}, f32[128,16]{0,1:T(8,128)S(1)}, u32[]{:S(2)}, u32[]{:S(2)}) collective-permute-start(f32[128,16]{0,1:T(8,128)S(1)} %bitcast.297), channel_id=1, source_target_pairs={{16,0},{17,1},{18,2},{19,3},{20,4},{21,5},{22,6},{23,7},{24,8},{25... | collective-permute-start | bytes 24584 | tf_op jit(solution)/shard_map/ppermute | solution.py:15
  73.4 73.8 %collective-permute-start.14 = (f32[128,16]{0,1:T(8,128)}, f32[128,16]{0,1:T(8,128)S(1)}, u32[]{:S(2)}, u32[]{:S(2)}) collective-permute-start(f32[128,16]{0,1:T(8,128)} %bitcast_reduce_fusion), channel_id=1, source_target_pairs={{0,16},{1,17},{2,18},{3,19},{4,20},{5,21},{6,22},{7,23},{8,24},{9,... | collective-permute-start | bytes 24584 | tf_op jit(solution)/shard_map/ppermute | solution.py:15
  75.3 71.9 %collective-permute-start.15 = (f32[128,16]{0,1:T(8,128)}, f32[128,16]{0,1:T(8,128)S(1)}, u32[]{:S(2)}, u32[]{:S(2)}) collective-permute-start(f32[128,16]{0,1:T(8,128)} %bitcast_reduce_fusion), channel_id=1, source_target_pairs={{16,0},{17,1},{18,2},{19,3},{20,4},{21,5},{22,6},{23,7},{24,8},{25... | collective-permute-start | bytes 24584 | tf_op jit(solution)/shard_map/ppermute | solution.py:15
  76.6 71.3 %collective-permute-start.12 = (bf16[128,1024]{1,0:T(8,128)(2,1)}, bf16[128,1024]{1,0:T(8,128)(2,1)}, u32[]{:S(2)}, u32[]{:S(2)}) collective-permute-start(bf16[128,1024]{1,0:T(8,128)(2,1)} %get-tuple-element.396), channel_id=1, source_target_pairs={{0,16},{1,17},{2,18},{3,19},{4,20},{5,21},{6,22},{7,23},{8,24},{9,... | collective-permute-start | bytes 786440 | tf_op jit(solution)/shard_map/ppermute | solution.py:15
  81.8 66.0 %collective-permute-start.13 = (bf16[128,1024]{1,0:T(8,128)(2,1)}, bf16[128,1024]{1,0:T(8,128)(2,1)}, u32[]{:S(2)}, u32[]{:S(2)}) collective-permute-start(bf16[128,1024]{1,0:T(8,128)(2,1)} %get-tuple-element.396), channel_id=1, source_target_pairs={{16,0},{17,1},{18,2},{19,3},{20,4},{21,5},{22,6},{23,7},{24,8},{25... | collective-permute-start | bytes 786440 | tf_op jit(solution)/shard_map/ppermute | solution.py:15
  (8 other events, 27.0 us)
Sparse Core Ops, SparseCore 0:
  22.6 43.8 all-gather.1
  70.4 71.6 reduce-scatter.1
  149.7 19.4 all-reduce.1
